TPU v7x, 32 devices: a whole 2x2x4 slice. The times are simulated.
32 devices in a mesh: tm: 4 (over y, x), sky: 8 (over z, core).
Axes of the slice: x: 2, y: 2, z: 4, core: 2. Of those that a mesh axis runs over, the one named last changes fastest.
Arguments:
- residual: float32 [16384, 128], P(('tm', 'sky')), may hold values from -110 to 110
- obs_weight: float32 [16384, 128], P(('tm', 'sky')), may hold values from 0.5 to 2
- source_partials: float32 [5, 16384, 128], P(None, ('tm', 'sky')), may hold values from -1 to 1
- attitude_partials: float32 [16, 16384, 128], P(None, ('tm', 'sky')), may hold values from -1.5 to 1.5
- source_index: int32 [16384, 128], P(('tm', 'sky')), may hold values from 0 to 127
- tile_pixel: int32 [16384], P(('tm', 'sky')), may hold values from 0 to 1023, as said below
- tile_knot: int32 [16384], P(('tm', 'sky')), may hold values from 0 to 2047, as said below
- pixel_slot: int32 [1024], replicated, may hold values from 0 to 1023, as said below
Outputs:
- final_residual: float32 [16384, 128], P(('tm', 'sky'))
- source_update: float32 [5, 131072], P(None, 'sky')
- attitude_update: float32 [4, 2048], P(None, 'tm')
Inputs may be any that keep to these rules, and one draw needn't show every extreme that they name: Tiles come in aligned blocks of 512; with owner = pixel_slot[tile_pixel[t]] // 128, no block holds more than 192 tiles of one owner, and every block holds exactly 192 tiles of some owner. `pixel_slot`: every slot number appears once. `tile_knot`: the tiles of aligned block q of 512 tiles have first knots in [q * 64, (q + 1) * 64).
All inputs are finite; a program needn't handle non-finite values.
Results may differ from a plain program's by a relative error of at most 0.0003.
Values sent between devices are 32-bit elements; how exact they have to be, the bound alone decides.
No kernel may reach another device: no remote copies, remote signals or barrier semaphores. Data moves between devices by JAX's collectives and lax.ppermute only.
A program may use at most 128 MiB of HBM per device.

v0:
```python
import math
import jax
import jax.numpy as jnp
from jax import lax
from jax.sharding import PartitionSpec as P

PIX_DEV = 128
SRC_PIX = 128
KNOTS_DEV = 512
SOURCE_PAIRS = tuple(((first, second) for first in range(5) for second in range(first, 5)))
KNOT_PAIRS = tuple(((first, second) for first in range(4) for second in range(first, 4)))


def passed_along(value, axis, steps):
    count = lax.axis_size(axis)
    first, last = (max(0, -steps), min(count, count - steps))
    return lax.ppermute(value, axis, [(source, source + steps) for source in range(first, last)])


def damped_solve(normal, target, order, pairs):
    entries = {}
    for number, couple in enumerate(pairs):
        entries[couple] = normal[number]
    factor = {}
    for column in range(order):
        pivot_value = entries[column, column] + 1.0
        for earlier in range(column):
            pivot_value = pivot_value - factor[column, earlier] * factor[column, earlier]
        pivot_value = jnp.sqrt(pivot_value)
        factor[column, column] = pivot_value
        for below in range(column + 1, order):
            current = entries[column, below]
            for earlier in range(column):
                current = current - factor[below, earlier] * factor[column, earlier]
            factor[below, column] = current / pivot_value
    forward = []
    for column in range(order):
        current = target[column]
        for earlier in range(column):
            current = current - factor[column, earlier] * forward[earlier]
        forward.append(current / factor[column, column])
    answer = [None] * order
    for column in reversed(range(order)):
        current = forward[column]
        for later in range(column + 1, order):
            current = current - factor[later, column] * answer[later]
        answer[column] = current / factor[column, column]
    return jnp.stack(answer)


def knot_terms(weights, partials, baseline):
    result = []
    for segment in range(4):
        portion = partials[4 * segment : 4 * segment + 4]
        sums_rows = [
            jnp.sum(weights * portion[first] * portion[second], axis=-1)
            for first, second in KNOT_PAIRS
        ]
        sums_rows = sums_rows + [
            jnp.sum(weights * portion[first] * baseline, axis=-1) for first in range(4)
        ]
        result.append(jnp.stack(sums_rows))
    return result


def correct(baseline, partials, picked):
    accumulated = partials[0] * picked[0]
    for component in range(1, partials.shape[0]):
        accumulated = accumulated + partials[component] * picked[component]
    return baseline - accumulated


def pixel_sums(products, indices, owners, capacity):

    def add_sender(sender, running):
        offset = sender * capacity
        portion = lax.dynamic_slice_in_dim(products, offset, capacity, 1)
        chosen = lax.dynamic_slice_in_dim(indices, offset, capacity, 0)
        within = ((chosen % SRC_PIX)[:, :, None] == jnp.arange(SRC_PIX, dtype=jnp.int32)).astype(
            jnp.float32
        )
        pixel_hits = (
            (chosen[:, 0] // SRC_PIX)[:, None] == jnp.arange(PIX_DEV, dtype=jnp.int32)
        ).astype(jnp.float32)
        spread = jnp.einsum("ctk,tks->cts", portion, within, precision=lax.Precision.HIGHEST)
        return running + jnp.einsum(
            "cts,tp->cps", spread, pixel_hits, precision=lax.Precision.HIGHEST
        )

    running = lax.fori_loop(0, owners, add_sender, jnp.zeros((20, PIX_DEV, SRC_PIX), jnp.float32))
    return running.reshape(20, PIX_DEV * SRC_PIX)


def pick_sources(update, indices, rows):
    pixels = update.shape[1] // SRC_PIX
    table = update.reshape(update.shape[0], pixels, SRC_PIX)
    blocks = indices.shape[0] // rows

    def fill(number, output):
        offset = number * rows
        chosen = lax.dynamic_slice_in_dim(indices, offset, rows, 0)
        pixel_hits = (
            (chosen[:, 0] // SRC_PIX)[:, None] == jnp.arange(pixels, dtype=jnp.int32)
        ).astype(jnp.float32)
        within = ((chosen % SRC_PIX)[:, :, None] == jnp.arange(SRC_PIX, dtype=jnp.int32)).astype(
            jnp.float32
        )
        row_values = jnp.einsum("tp,cps->cts", pixel_hits, table, precision=lax.Precision.HIGHEST)
        picked = jnp.einsum("cts,tks->ctk", row_values, within, precision=lax.Precision.HIGHEST)
        return lax.dynamic_update_slice_in_dim(output, picked, offset, 1)

    empty = jnp.zeros((update.shape[0], indices.shape[0], indices.shape[1]), jnp.float32)
    return lax.fori_loop(0, blocks, fill, empty)


def body(
    residual,
    obs_weight,
    source_partials,
    attitude_partials,
    source_index,
    tile_pixel,
    tile_knot,
    pixel_slot,
):
    owners = lax.axis_size("sky")
    tiles = residual.shape[0]
    capacity = 3 * tiles // owners
    pixels = pixel_slot.shape[0]
    pixel_match = (tile_pixel[:, None] == jnp.arange(pixels, dtype=jnp.int32)[None, :]).astype(
        jnp.float32
    )
    seats_float = jnp.dot(
        pixel_match, pixel_slot.astype(jnp.float32), precision=lax.Precision.HIGHEST
    )
    seats = seats_float.astype(jnp.int32)
    owner_ids = seats // PIX_DEV
    local_pixel = seats % PIX_DEV
    member = (owner_ids[:, None] == jnp.arange(owners, dtype=jnp.int32)[None, :]).astype(
        jnp.float32
    )
    tile_numbers = jnp.arange(tiles, dtype=jnp.int32)
    lower = (tile_numbers[:, None] > tile_numbers[None, :]).astype(jnp.float32)
    before = jnp.dot(lower, member, precision=lax.Precision.HIGHEST)
    position = jnp.sum(before * member, axis=1).astype(jnp.int32)
    slot_index = owner_ids * capacity + position
    place = (jnp.arange(owners * capacity, dtype=jnp.int32)[:, None] == slot_index[None, :]).astype(
        jnp.float32
    )
    local_source = (local_pixel[:, None] * SRC_PIX + source_index).astype(jnp.float32)
    sent_index = jnp.dot(place, local_source, precision=lax.Precision.HIGHEST).astype(jnp.int32)[
        None
    ]
    root_weight = jnp.sqrt(obs_weight)
    fields = jnp.concatenate(
        [(root_weight * residual)[None], root_weight[None] * source_partials], axis=0
    )
    packed = jnp.einsum("st,ctk->csk", place, fields, precision=lax.Precision.HIGHEST)
    arrived, arrived_index = (
        lax.all_to_all(packed, "sky", split_axis=1, concat_axis=1, tiled=True),
        lax.all_to_all(sent_index, "sky", split_axis=1, concat_axis=1, tiled=True),
    )
    scaled = arrived[1:]
    products = [scaled[first] * scaled[second] for first, second in SOURCE_PAIRS]
    products = jnp.stack(products + [scaled[first] * arrived[0] for first in range(5)])
    normals = pixel_sums(products, arrived_index[0], owners, capacity)
    summed = lax.psum(normals, "tm")
    source_update = damped_solve(summed[:15], summed[15:], 5, SOURCE_PAIRS)
    everything = lax.all_gather(source_update, "sky", axis=1, tiled=True)
    global_source = seats[:, None] * SRC_PIX + source_index
    picked = pick_sources(everything, global_source, math.gcd(tiles, 64))
    settled = correct(residual, source_partials, picked)
    knot_start = tile_knot - lax.axis_index("tm") * KNOTS_DEV
    knot_hits = (knot_start[:, None] == jnp.arange(KNOTS_DEV, dtype=jnp.int32)[None, :]).astype(
        jnp.float32
    )
    accumulated = jnp.zeros((14, KNOTS_DEV + 3), jnp.float32)
    for segment, tile_sums in enumerate(knot_terms(obs_weight, attitude_partials, settled)):
        placed = jnp.dot(tile_sums, knot_hits, precision=lax.Precision.HIGHEST)
        accumulated = accumulated + jnp.pad(placed, ((0, 0), (segment, 3 - segment)))
    arriving = passed_along(accumulated[:, KNOTS_DEV:], "tm", 1)
    own_rows = accumulated[:, :KNOTS_DEV] + jnp.pad(arriving, ((0, 0), (0, KNOTS_DEV - 3)))
    whole = lax.psum(own_rows, "sky")
    attitude_update = damped_solve(whole[:10], whole[10:], 4, KNOT_PAIRS)
    following = passed_along(attitude_update[:, :3], "tm", -1)
    extended = jnp.concatenate([attitude_update, following], axis=1)
    accumulated_fix = None
    for segment in range(4):
        window = extended[:, segment : segment + KNOTS_DEV]
        values = jnp.dot(window, knot_hits.T, precision=lax.Precision.HIGHEST)
        for component in range(4):
            addend = attitude_partials[4 * segment + component] * values[component][:, None]
            accumulated_fix = addend if accumulated_fix is None else accumulated_fix + addend
    final_residual = settled - accumulated_fix
    return (final_residual, source_update, attitude_update)


def solution(mesh):
    in_specs = (
        P(("tm", "sky"), None),
        P(("tm", "sky"), None),
        P(None, ("tm", "sky"), None),
        P(None, ("tm", "sky"), None),
        P(("tm", "sky"), None),
        P(("tm", "sky")),
        P(("tm", "sky")),
        P(),
    )
    out_specs = (P(("tm", "sky"), None), P(None, "sky"), P(None, "tm"))
    return jax.shard_map(body, mesh=mesh, in_specs=in_specs, out_specs=out_specs, check_vma=False)
```

profile of v0, /device:TPU:0, one launch (start us, length us, event | category | flops | bytes accessed | tf_op | source)
XLA Modules:
  0.0 626.5 jit_solution(8565217620249601764)
XLA Ops:
  12.9 6.0 convolution_bitcast_fusion.1
  18.8 6.2 copy.44
  25.0 6.5 %all-to-all-start.1 = ((f32[6,1536,128]{2,0,1:T(8,128)}), f32[6,1536,128]{2,0,1:T(8,128)}, u32[]{:S(2)}, u32[]{:S(2)}) async-start(f32[6,1536,128]{2,0,1:T(8,128)} %copy.44), calls=%async_computation.1 | async-start | bytes 12582912 | tf_op jit(solution)/shard_map/all_to_all | solution.py:160
  34.0 136.5 %all-to-all-done.1 = f32[6,1536,128]{2,0,1:T(8,128)} async-done(((f32[6,1536,128]{2,0,1:T(8,128)}), f32[6,1536,128]{2,0,1:T(8,128)}, u32[]{:S(2)}, u32[]{:S(2)}) %all-to-all-start.1) | async-done | bytes 4718624 | tf_op jit(solution)/shard_map/all_to_all | solution.py:160
  175.0 22.1 %slice_multiply_fusion = (f32[1,1536,128]{2,0,1:T(1,128)S(1)}, f32[1,1536,128]{2,0,1:T(1,128)S(1)}, f32[1,1536,128]{2,0,1:T(1,128)}, f32[1,1536,128]{2,0,1:T(1,1...) fusion(f32[6,1536,128]{2,0,1:T(8,128)} %all-to-all-done.1), kind=kLoop, calls=%fused_computation.340 | loop fusion | flops 2359296 | bytes 14155776 | tf_op jit(solution)/shard_map/mul | solution.py:165
  197.1 20.9 %slice_multiply_fusion.1 = (f32[1,1536,128]{2,0,1:T(1,128)}, f32[1,1536,128]{2,0,1:T(1,128)}, f32[1,1536,128]{2,0,1:T(1,128)}, f32[1,1536,128]{2,0,1:T(1,128)}, ...) fusion(f32[6,1536,128]{2,0,1:T(8,128)} %all-to-all-done.1), kind=kLoop, calls=%fused_computation.341 | loop fusion | flops 1572864 | bytes 11010048 | tf_op jit(solution)/shard_map/mul | solution.py:165
  218.0 49.6 %stack.218 = f32[20,1536,128]{2,0,1:T(8,128)} concatenate(f32[1,1536,128]{2,0,1:T(1,128)} %get-tuple-element.400, f32[1,1536,128]{2,0,1:T(1,128)} %get-tuple-element.408, f32[1,1536,128]{2,0,1:T(1,128)} %get-tuple-element.407, f32[1,1536,128]{2,0,1:T(1,128)} %get-tuple-element.406, f32[1,1536,128]{2,0,1:T(1,128)} %get-tuple-element.405, f32[1,1536,128]{2,0,1:T(1,128)S(1)} %get-tuple-element.390, ...), dimensions={0} | concatenate | bytes 31457280 | tf_op jit(solution)/shard_map/stack | solution.py:165
  267.7 114.9 %while.32 = (s32[]{:T(128)}, f32[20,128,128]{2,1,0:T(8,128)S(1)}, s32[1536,128]{1,0:T(8,128)}, f32[20,1536,128]{2,0,1:T(8,128)}, s32[]{:T(128)}, /*index=5*/s32[]{:T(128)}, s32[]{:T(128)}, s32[]{:T(128)}) while((s32[]{:T(128)}, f32[20,128,128]{2,1,0:T(8,128)S(1)}, s32[1536,128]{1,0:T(8,128)}, f32[20,1536,128]{2,0,1:T(8,128)}, ...), condition=%wide.region_2.3_spmd.clone, body=%wide.region_1.2_spmd.clone.sunk | while | flops 1514048256 | bytes 9800085 | solution.py:90
  268.8 9.9 %fusion.206 = f32[20,192,128]{2,0,1:T(8,128)} fusion(f32[20,1536,128]{2,0,1:T(8,128)} %get-tuple-element.501, s32[]{:T(128)S(6)} %select_n.124, s32[192,128]{1,0:T(8,128)S(1)} %copy.140), kind=kOutput, calls=%fused_computation.26.clone.1 | convolution fusion | flops 758120448 | bytes 4423684 | tf_op jit(solution)/shard_map/while/body/eval_jaxpr/ctk,tks->cts/dot_general | solution.py:85
  283.2 9.9 %fusion.206 = f32[20,192,128]{2,0,1:T(8,128)} fusion(f32[20,1536,128]{2,0,1:T(8,128)} %get-tuple-element.501, s32[]{:T(128)S(6)} %select_n.124, s32[192,128]{1,0:T(8,128)S(1)} %copy.140), kind=kOutput, calls=%fused_computation.26.clone.1 | convolution fusion | flops 758120448 | bytes 4423684 | tf_op jit(solution)/shard_map/while/body/eval_jaxpr/ctk,tks->cts/dot_general | solution.py:85
  297.6 9.9 %fusion.206 = f32[20,192,128]{2,0,1:T(8,128)} fusion(f32[20,1536,128]{2,0,1:T(8,128)} %get-tuple-element.501, s32[]{:T(128)S(6)} %select_n.124, s32[192,128]{1,0:T(8,128)S(1)} %copy.140), kind=kOutput, calls=%fused_computation.26.clone.1 | convolution fusion | flops 758120448 | bytes 4423684 | tf_op jit(solution)/shard_map/while/body/eval_jaxpr/ctk,tks->cts/dot_general | solution.py:85
  311.9 9.9 %fusion.206 = f32[20,192,128]{2,0,1:T(8,128)} fusion(f32[20,1536,128]{2,0,1:T(8,128)} %get-tuple-element.501, s32[]{:T(128)S(6)} %select_n.124, s32[192,128]{1,0:T(8,128)S(1)} %copy.140), kind=kOutput, calls=%fused_computation.26.clone.1 | convolution fusion | flops 758120448 | bytes 4423684 | tf_op jit(solution)/shard_map/while/body/eval_jaxpr/ctk,tks->cts/dot_general | solution.py:85
  326.3 9.9 %fusion.206 = f32[20,192,128]{2,0,1:T(8,128)} fusion(f32[20,1536,128]{2,0,1:T(8,128)} %get-tuple-element.501, s32[]{:T(128)S(6)} %select_n.124, s32[192,128]{1,0:T(8,128)S(1)} %copy.140), kind=kOutput, calls=%fused_computation.26.clone.1 | convolution fusion | flops 758120448 | bytes 4423684 | tf_op jit(solution)/shard_map/while/body/eval_jaxpr/ctk,tks->cts/dot_general | solution.py:85
  340.6 9.9 %fusion.206 = f32[20,192,128]{2,0,1:T(8,128)} fusion(f32[20,1536,128]{2,0,1:T(8,128)} %get-tuple-element.501, s32[]{:T(128)S(6)} %select_n.124, s32[192,128]{1,0:T(8,128)S(1)} %copy.140), kind=kOutput, calls=%fused_computation.26.clone.1 | convolution fusion | flops 758120448 | bytes 4423684 | tf_op jit(solution)/shard_map/while/body/eval_jaxpr/ctk,tks->cts/dot_general | solution.py:85
  355.0 9.9 %fusion.206 = f32[20,192,128]{2,0,1:T(8,128)} fusion(f32[20,1536,128]{2,0,1:T(8,128)} %get-tuple-element.501, s32[]{:T(128)S(6)} %select_n.124, s32[192,128]{1,0:T(8,128)S(1)} %copy.140), kind=kOutput, calls=%fused_computation.26.clone.1 | convolution fusion | flops 758120448 | bytes 4423684 | tf_op jit(solution)/shard_map/while/body/eval_jaxpr/ctk,tks->cts/dot_general | solution.py:85
  369.4 9.9 %fusion.206 = f32[20,192,128]{2,0,1:T(8,128)} fusion(f32[20,1536,128]{2,0,1:T(8,128)} %get-tuple-element.501, s32[]{:T(128)S(6)} %select_n.124, s32[192,128]{1,0:T(8,128)S(1)} %copy.140), kind=kOutput, calls=%fused_computation.26.clone.1 | convolution fusion | flops 758120448 | bytes 4423684 | tf_op jit(solution)/shard_map/while/body/eval_jaxpr/ctk,tks->cts/dot_general | solution.py:85
  385.1 61.7 %all-reduce.7.cloned.1.call-done = f32[20,16384]{1,0:T(8,128)} async-done(((f32[20,16384]{1,0:T(8,128)}), f32[20,16384]{1,0:T(8,128)}) %all-reduce.7.cloned.1.call-update) | async-done | bytes 1310736 | tf_op jit(solution)/shard_map/psum | solution.py:167
  446.8 5.2 fusion.141
  468.1 40.0 %all-gather.2.cloned.1.call-done = f32[5,131072]{1,0:T(8,128)} async-done(((f32[5,16384]{1,0:T(8,128)}), f32[5,131072]{1,0:T(8,128)}) %all-gather.2.cloned.1.call-update) | async-done | bytes 2621456 | tf_op jit(solution)/shard_map/all_gather | solution.py:169
  511.9 55.2 %while.31 = (s32[]{:T(128)}, f32[5,512,128]{2,1,0:T(8,128)}, s32[512,128]{0,1:T(8,128)S(1)}, f32[5,1024,128]{2,1,0:T(8,128)S(1)}, s32[]{:T(128)}, /*index=5*/s32[]{:T(128)}, s32[]{:T(128)}, s32[]{:T(128)}) while((s32[]{:T(128)}, f32[5,512,128]{2,1,0:T(8,128)}, s32[512,128]{0,1:T(8,128)S(1)}, f32[5,1024,128]{2,1,0:T(8,128)S(1)}, s32[]{:T(128)}, ...), condition=%wide.region_5.6_spmd, body=%wide.region_4.5_spmd.sunk | while | flops 567436224 | bytes 3605391 | solution.py:113
  513.4 4.8 fusion.202
  527.1 4.8 fusion.202
  534.1 4.8 fusion.202
  580.5 25.9 %psum.15 = f32[14,512]{1,0:T(8,128)S(1)} all-reduce(f32[14,512]{1,0:T(8,128)S(1)} %slice_add_fusion.5), channel_id=1, replica_groups=mesh['tm'=4,'sky'=8] {'sky'}, use_global_device_ids=true, to_apply=%region_62.63 | all-reduce | flops 7168 | bytes 57344 | tf_op jit(solution)/shard_map/psum | solution.py:183
  (177 shorter events, 137.0 us)
Async XLA Ops:
  7.2 5.1 copy-start.1
  25.0 6.5 %copy-start.8 = (s32[512,128]{1,0:T(8,128)S(1)}, s32[512,128]{1,0:T(8,128)}, u32[]{:S(2)}) copy-start(s32[512,128]{1,0:T(8,128)} %param.16) | copy-start | bytes 786436
  25.0 145.5 %all-to-all-start.1 = ((f32[6,1536,128]{2,0,1:T(8,128)}), f32[6,1536,128]{2,0,1:T(8,128)}, u32[]{:S(2)}, u32[]{:S(2)}) async-start(f32[6,1536,128]{2,0,1:T(8,128)} %copy.44), calls=%async_computation.1 | async-start | bytes 12582912 | tf_op jit(solution)/shard_map/all_to_all | solution.py:160
  170.5 97.1 %all-to-all-start = ((s32[1,1536,128]{2,0,1:T(1,128)}), s32[1,1536,128]{2,0,1:T(1,128)}, u32[]{:S(2)}, u32[]{:S(2)}) async-start(s32[1,1536,128]{2,0,1:T(1,128)} %bitcast.7), calls=%async_computation | async-start | bytes 1572864 | tf_op jit(solution)/shard_map/all_to_all | solution.py:161
  174.7 272.1 %all-reduce.7.cloned.1.call-start = ((), (), s32[]{:S(2)}) async-start(), calls=%async_computation.2 | async-start | bytes 3145728 | tf_op jit(solution)/shard_map/psum | solution.py:167
  384.8 123.3 %all-gather.2.cloned.1.call-start = ((), (), s32[]{:S(2)}) async-start(), calls=%async_computation.3 | async-start | bytes 4718592 | tf_op jit(solution)/shard_map/all_gather | solution.py:169
  456.0 5.2 copy-start.10
  456.0 5.3 copy-start.2
  567.1 3.7 copy-start
  567.1 3.7 copy-start.3
  567.1 3.8 copy-start.4
  567.1 3.9 copy-start.5
  567.1 3.9 copy-start.6
  567.1 4.0 copy-start.7
  575.8 4.7 collective-permute-start
  606.6 13.0 %copy-start.9 = (f32[4,512]{1,0:T(4,128)}, f32[4,512]{1,0:T(4,128)S(1)}, u32[]{:S(2)}) copy-start(f32[4,512]{1,0:T(4,128)S(1)} %pad_maximum_fusion.1) | copy-start | bytes 24580
  607.3 5.7 collective-permute-start.1
Sparse Core Ops, SparseCore 0:
  384.9 61.8 all-reduce.6
  461.2 46.8 all-gather.1
where the time goes:
time: 634 us; the launch traced here: 626 us
  waiting for transfers between devices  244 us (38%)
  matrix products  168 us (26%)
  local copies, waits for them, and re-layouts  81.4 us (13%)
  other arithmetic  76.7 us (12%)
  blocking collectives  25.9 us (4%)
  starting transfers between devices  15.8 us (2%)
  between operations  14.4 us (2%)
    all_to_all x1, waiting for transfers between devices, body(): lax.all_to_all(packed, 'sky', split_axis=1, concat_axis=1, tiled=True)  137 us
    dot_general x8, matrix products, add_sender(): jnp.einsum('ctk,tks->cts', portion, within, precision=lax.Precision.HIGHEST)  79.5 us
    psum x1, waiting for transfers between devices, body(): summed = lax.psum(normals, 'tm')  61.7 us
    another operation x1, local copies, waits for them, and re-layouts, body(): jnp.stack(products + [scaled[first] * arrived[0] for first in range(5)])  49.6 us
    mul x2, other arithmetic, body(): scaled[first] * arrived[0]  43.1 us
    all_gather x1, waiting for transfers between devices, body(): everything = lax.all_gather(source_update, 'sky', axis=1, tiled=True)  40 us
    dot_general x8, matrix products, fill(): jnp.einsum('cts,tks->ctk', row_values, within, precision=lax.Precision.HI...  38 us
    psum x1, blocking collectives, body(): whole = lax.psum(own_rows, 'sky')  25.9 us
  transfers between devices with their start and end apart: 6, of which 5 were waited for; matrix products, arithmetic and copies ran while one was open for 16% of the time, Pallas kernels for 0%

commit v1 on v0

--- a/solution.py
+++ b/solution.py
@@ -1,3 +1,4 @@
+import functools
 import math
 import jax
 import jax.numpy as jnp
@@ -9,6 +10,38 @@
 KNOTS_DEV = 512
 SOURCE_PAIRS = tuple(((first, second) for first in range(5) for second in range(first, 5)))
 KNOT_PAIRS = tuple(((first, second) for first in range(4) for second in range(first, 4)))
+
+
+def object_make(piece_in, ndim_at, array_in):
+    x_new, y1 = (piece_in.shape[:ndim_at], piece_in.shape[ndim_at + 1 :])
+    taken_in = jnp.moveaxis(piece_in.reshape(*x_new, array_in, -1, *y1), ndim_at, 0)
+    return taken_in
+
+
+def wrap_frames(shard_in, d0):
+    u_next = list(shard_in.shape[1:])
+    u_next[d0] *= shard_in.shape[0]
+    e_now = jnp.moveaxis(shard_in, 0, d0).reshape(u_next)
+    return e_now
+
+
+def pools_edit(incoming_x, along_axis, slab_in, q_in):
+    v1 = lax.axis_size(along_axis)
+    vec_out = lax.axis_index(along_axis)
+    outer, f_next = (v1, vec_out)
+    local_part = object_make(incoming_x, slab_in, outer)
+    arrivals = [local_part[f_next]]
+    for d in range(1, outer):
+        value_now = local_part[f_next ^ d]
+        arrivals.append(
+            lax.ppermute(value_now, axis_name=along_axis, perm=[(u, u ^ d) for u in range(outer)])
+        )
+    local_part = jnp.stack(arrivals, 0)[f_next ^ jnp.arange(outer)]
+    local_out = wrap_frames(local_part, q_in)
+    return local_out
+
+
+read_target_on_mesh = functools.partial(pools_edit, along_axis="sky", slab_in=1, q_in=1)
 
 
 def passed_along(value, axis, steps):
@@ -157,7 +190,7 @@
     )
     packed = jnp.einsum("st,ctk->csk", place, fields, precision=lax.Precision.HIGHEST)
     arrived, arrived_index = (
-        lax.all_to_all(packed, "sky", split_axis=1, concat_axis=1, tiled=True),
+        read_target_on_mesh(packed),
         lax.all_to_all(sent_index, "sky", split_axis=1, concat_axis=1, tiled=True),
     )
     scaled = arrived[1:]

time: 634 us -> 586 us (0.924)
  waiting for transfers between devices: 244 us -> 201 us
  other arithmetic: 76.7 us -> 42 us
  local copies, waits for them, and re-layouts: 81.4 us -> 105 us
    all_to_all x1 -> x0, waiting for transfers between devices: 137 us -> none  [body(): lax.all_to_all(packed, 'sky', split_axis=1, concat_axis=1, tiled=True)]
    ppermute x0 -> x7, waiting for transfers between devices: none -> 64.7 us  [pools_edit(): lax.ppermute(value_now, axis_name=along_axis, perm=[(u, u ^ d) for u in r...]
    mul x2, other arithmetic: 43.1 us -> 8.47 us  [body(): scaled[first] * arrived[0]]
    psum x1, waiting for transfers between devices: 61.7 us -> 91 us  [body(): summed = lax.psum(normals, 'tm')]
    unnamed x29 -> x38, local copies, waits for them, and re-layouts: 8.03 us -> 21.8 us
    ppermute x0 -> x7, starting transfers between devices: none -> 10.1 us  [pools_edit(): lax.ppermute(value_now, axis_name=along_axis, perm=[(u, u ^ d) for u in r...]
    all_to_all x1 -> x0, starting transfers between devices: 6.49 us -> none  [body(): lax.all_to_all(packed, 'sky', split_axis=1, concat_axis=1, tiled=True)]
  transfers between devices with their start and end apart: 6 -> 12, of which waited for: 5 -> 8; matrix products, arithmetic and copies ran while one was open for 16% -> 15% of each run, Pallas kernels for 0% -> 0%
where the time goes in v1:
time: 586 us; the launch traced here: 577 us
  waiting for transfers between devices  201 us (34%)
  matrix products  168 us (29%)
  local copies, waits for them, and re-layouts  105 us (18%)
  other arithmetic  42 us (7%)
  blocking collectives  25.9 us (4%)
  starting transfers between devices  20 us (3%)
  between operations  14.4 us (2%)
    psum x1, waiting for transfers between devices, body(): summed = lax.psum(normals, 'tm')  91 us
    dot_general x8, matrix products, add_sender(): jnp.einsum('ctk,tks->cts', portion, within, precision=lax.Precision.HIGHEST)  79.5 us
    ppermute x7, waiting for transfers between devices, pools_edit(): lax.ppermute(value_now, axis_name=along_axis, perm=[(u, u ^ d) for u in r...  64.7 us
    another operation x1, local copies, waits for them, and re-layouts, body(): jnp.stack(products + [scaled[first] * arrived[0] for first in range(5)])  49.6 us
    all_gather x1, waiting for transfers between devices, body(): everything = lax.all_gather(source_update, 'sky', axis=1, tiled=True)  40 us
    dot_general x8, matrix products, fill(): jnp.einsum('cts,tks->ctk', row_values, within, precision=lax.Precision.HI...  38 us
    psum x1, blocking collectives, body(): whole = lax.psum(own_rows, 'sky')  25.9 us
    dot_general x8, matrix products, add_sender(): jnp.einsum('cts,tp->cps', spread, pixel_hits, precision=lax.Precision.HIG...  25.8 us
  transfers between devices with their start and end apart: 12, of which 8 were waited for; matrix products, arithmetic and copies ran while one was open for 15% of the time, Pallas kernels for 0%

profile of v1, /device:TPU:0, one launch (start us, length us, event | category | flops | bytes accessed | tf_op | source)
XLA Modules:
  0.0 577.3 jit_solution(4861496219282790001)
XLA Ops:
  14.1 6.1 %convolution_bitcast_fusion.1 = f32[6,1536,128]{1,2,0:T(8,128)} fusion(f32[5,512,128]{1,2,0:T(8,128)S(1)} %broadcast_multiply_fusion, f32[1,512,128]{1,2,0:T(8,128)S(1)} %get-tuple-element.414, s32[512]{0:T(512)S(1)} %convert_add_fusion), kind=kOutput, calls=%fused_computation.43 | convolution fusion | flops 7248936960 | bytes 6293504 | tf_op jit(solution)/shard_map/st,ctk->csk/dot_general | solution.py:191
  20.2 6.0 %copy.43 = f32[6,1536,128]{2,1,0:T(8,128)} copy(f32[6,1536,128]{1,2,0:T(8,128)} %convolution_bitcast_fusion.1) | data formatting | bytes 9437184 | tf_op jit(solution)/shard_map/st,ctk->csk/transpose | solution.py:191
  38.4 4.9 all-to-all-start
  51.1 21.3 %collective-permute-done.1 = f32[6,192,128]{2,1,0:T(8,128)} collective-permute-done((f32[6,192,128]{2,1,0:T(8,128)}, f32[6,192,128]{2,1,0:T(8,128)}, u32[]{:S(2)}, u32[]{:S(2)}) %collective-permute-start.1) | collective-permute-done | bytes 589856 | tf_op jit(solution)/shard_map/ppermute | solution.py:37
  74.8 9.8 %collective-permute-done.2 = f32[6,192,128]{2,1,0:T(8,128)} collective-permute-done((f32[6,192,128]{2,1,0:T(8,128)}, f32[6,192,128]{2,1,0:T(8,128)}, u32[]{:S(2)}, u32[]{:S(2)}) %collective-permute-start.2) | collective-permute-done | bytes 589856 | tf_op jit(solution)/shard_map/ppermute | solution.py:37
  90.4 22.8 %collective-permute-done.5 = f32[6,192,128]{2,1,0:T(8,128)S(1)} collective-permute-done((f32[6,192,128]{2,1,0:T(8,128)S(1)}, f32[6,192,128]{2,1,0:T(8,128)S(1)}, u32[]{:S(2)}, u32[]{:S(2)}) %collective-permute-start.5) | collective-permute-done | bytes 589856 | tf_op jit(solution)/shard_map/ppermute | solution.py:37
  114.1 10.8 %collective-permute-done.6 = f32[6,192,128]{2,1,0:T(8,128)S(1)} collective-permute-done((f32[6,192,128]{2,1,0:T(8,128)S(1)}, f32[6,192,128]{2,1,0:T(8,128)S(1)}, u32[]{:S(2)}, u32[]{:S(2)}) %collective-permute-start.6) | collective-permute-done | bytes 589856 | tf_op jit(solution)/shard_map/ppermute | solution.py:37
  125.8 5.3 gather_fusion
  131.2 5.3 slice_multiply_fusion.1
  139.6 49.6 %stack.250 = f32[20,1536,128]{2,0,1:T(8,128)} concatenate(f32[1,1536,128]{2,0,1:T(1,128)} %bitcast.530, f32[1,1536,128]{2,0,1:T(1,128)} %bitcast.538, f32[1,1536,128]{2,0,1:T(1,128)} %bitcast.537, f32[1,1536,128]{2,0,1:T(1,128)} %bitcast.536, f32[1,1536,128]{2,0,1:T(1,128)} %bitcast.535, f32[1,1536,128]{2,0,1:T(1,128)S(1)} %bitcast.520, f32[1,1536,128]{2,0,1:T(1,128)} %bitcast.521, ...), dimensions={0} | concatenate | bytes 31457280 | tf_op jit(solution)/shard_map/stack | solution.py:198
  189.3 114.9 %while.32 = (s32[]{:T(128)}, f32[20,128,128]{2,1,0:T(8,128)S(1)}, s32[1536,128]{1,0:T(8,128)}, f32[20,1536,128]{2,0,1:T(8,128)}, s32[]{:T(128)}, /*index=5*/s32[]{:T(128)}, s32[]{:T(128)}, s32[]{:T(128)}) while((s32[]{:T(128)}, f32[20,128,128]{2,1,0:T(8,128)S(1)}, s32[1536,128]{1,0:T(8,128)}, f32[20,1536,128]{2,0,1:T(8,128)}, ...), condition=%wide.region_2.3_spmd.clone, body=%wide.region_1.2_spmd.clone.sunk | while | flops 1514048256 | bytes 9800085 | solution.py:123
  190.4 9.9 %fusion.207 = f32[20,192,128]{2,0,1:T(8,128)} fusion(f32[20,1536,128]{2,0,1:T(8,128)} %get-tuple-element.504, s32[]{:T(128)S(6)} %select_n.170, s32[192,128]{1,0:T(8,128)S(1)} %copy.159), kind=kOutput, calls=%fused_computation.27.clone.1 | convolution fusion | flops 758120448 | bytes 4423684 | tf_op jit(solution)/shard_map/while/body/eval_jaxpr/ctk,tks->cts/dot_general | solution.py:118
  204.8 9.9 %fusion.207 = f32[20,192,128]{2,0,1:T(8,128)} fusion(f32[20,1536,128]{2,0,1:T(8,128)} %get-tuple-element.504, s32[]{:T(128)S(6)} %select_n.170, s32[192,128]{1,0:T(8,128)S(1)} %copy.159), kind=kOutput, calls=%fused_computation.27.clone.1 | convolution fusion | flops 758120448 | bytes 4423684 | tf_op jit(solution)/shard_map/while/body/eval_jaxpr/ctk,tks->cts/dot_general | solution.py:118
  219.1 9.9 %fusion.207 = f32[20,192,128]{2,0,1:T(8,128)} fusion(f32[20,1536,128]{2,0,1:T(8,128)} %get-tuple-element.504, s32[]{:T(128)S(6)} %select_n.170, s32[192,128]{1,0:T(8,128)S(1)} %copy.159), kind=kOutput, calls=%fused_computation.27.clone.1 | convolution fusion | flops 758120448 | bytes 4423684 | tf_op jit(solution)/shard_map/while/body/eval_jaxpr/ctk,tks->cts/dot_general | solution.py:118
  233.5 9.9 %fusion.207 = f32[20,192,128]{2,0,1:T(8,128)} fusion(f32[20,1536,128]{2,0,1:T(8,128)} %get-tuple-element.504, s32[]{:T(128)S(6)} %select_n.170, s32[192,128]{1,0:T(8,128)S(1)} %copy.159), kind=kOutput, calls=%fused_computation.27.clone.1 | convolution fusion | flops 758120448 | bytes 4423684 | tf_op jit(solution)/shard_map/while/body/eval_jaxpr/ctk,tks->cts/dot_general | solution.py:118
  247.9 9.9 %fusion.207 = f32[20,192,128]{2,0,1:T(8,128)} fusion(f32[20,1536,128]{2,0,1:T(8,128)} %get-tuple-element.504, s32[]{:T(128)S(6)} %select_n.170, s32[192,128]{1,0:T(8,128)S(1)} %copy.159), kind=kOutput, calls=%fused_computation.27.clone.1 | convolution fusion | flops 758120448 | bytes 4423684 | tf_op jit(solution)/shard_map/while/body/eval_jaxpr/ctk,tks->cts/dot_general | solution.py:118
  262.2 9.9 %fusion.207 = f32[20,192,128]{2,0,1:T(8,128)} fusion(f32[20,1536,128]{2,0,1:T(8,128)} %get-tuple-element.504, s32[]{:T(128)S(6)} %select_n.170, s32[192,128]{1,0:T(8,128)S(1)} %copy.159), kind=kOutput, calls=%fused_computation.27.clone.1 | convolution fusion | flops 758120448 | bytes 4423684 | tf_op jit(solution)/shard_map/while/body/eval_jaxpr/ctk,tks->cts/dot_general | solution.py:118
  276.6 9.9 %fusion.207 = f32[20,192,128]{2,0,1:T(8,128)} fusion(f32[20,1536,128]{2,0,1:T(8,128)} %get-tuple-element.504, s32[]{:T(128)S(6)} %select_n.170, s32[192,128]{1,0:T(8,128)S(1)} %copy.159), kind=kOutput, calls=%fused_computation.27.clone.1 | convolution fusion | flops 758120448 | bytes 4423684 | tf_op jit(solution)/shard_map/while/body/eval_jaxpr/ctk,tks->cts/dot_general | solution.py:118
  291.0 9.9 %fusion.207 = f32[20,192,128]{2,0,1:T(8,128)} fusion(f32[20,1536,128]{2,0,1:T(8,128)} %get-tuple-element.504, s32[]{:T(128)S(6)} %select_n.170, s32[192,128]{1,0:T(8,128)S(1)} %copy.159), kind=kOutput, calls=%fused_computation.27.clone.1 | convolution fusion | flops 758120448 | bytes 4423684 | tf_op jit(solution)/shard_map/while/body/eval_jaxpr/ctk,tks->cts/dot_general | solution.py:118
  306.5 91.0 %all-reduce.7.cloned.1.call-done = f32[20,16384]{1,0:T(8,128)} async-done(((f32[20,16384]{1,0:T(8,128)}), f32[20,16384]{1,0:T(8,128)}) %all-reduce.7.cloned.1.call-update) | async-done | bytes 1310736 | tf_op jit(solution)/shard_map/psum | solution.py:200
  397.5 5.2 fusion.141
  418.9 40.0 %all-gather.2.cloned.1.call-done = f32[5,131072]{1,0:T(8,128)} async-done(((f32[5,16384]{1,0:T(8,128)}), f32[5,131072]{1,0:T(8,128)}) %all-gather.2.cloned.1.call-update) | async-done | bytes 2621456 | tf_op jit(solution)/shard_map/all_gather | solution.py:202
  462.8 55.2 %while.31 = (s32[]{:T(128)}, f32[5,512,128]{2,1,0:T(8,128)}, s32[512,128]{0,1:T(8,128)S(1)}, f32[5,1024,128]{2,1,0:T(8,128)S(1)}, s32[]{:T(128)}, /*index=5*/s32[]{:T(128)}, s32[]{:T(128)}, s32[]{:T(128)}) while((s32[]{:T(128)}, f32[5,512,128]{2,1,0:T(8,128)}, s32[512,128]{0,1:T(8,128)S(1)}, f32[5,1024,128]{2,1,0:T(8,128)S(1)}, s32[]{:T(128)}, ...), condition=%wide.region_5.6_spmd, body=%wide.region_4.5_spmd.sunk | while | flops 567436224 | bytes 3605391 | solution.py:146
  531.4 25.9 %psum.15 = f32[14,512]{1,0:T(8,128)S(1)} all-reduce(f32[14,512]{1,0:T(8,128)S(1)} %slice_add_fusion.5), channel_id=1, replica_groups=mesh['tm'=4,'sky'=8] {'sky'}, use_global_device_ids=true, to_apply=%region_62.63 | all-reduce | flops 7168 | bytes 57344 | tf_op jit(solution)/shard_map/psum | solution.py:216
  (204 shorter events, 178.8 us)
Async XLA Ops:
  26.2 9.7 %copy-start.7 = (s32[512,128]{1,0:T(8,128)S(1)}, s32[512,128]{1,0:T(8,128)}, u32[]{:S(2)}) copy-start(s32[512,128]{1,0:T(8,128)} %param.16) | copy-start | bytes 786436
  29.9 15.6 %collective-permute-start = (f32[6,192,128]{2,1,0:T(8,128)}, f32[6,192,128]{2,1,0:T(8,128)}, u32[]{:S(2)}, u32[]{:S(2)}) collective-permute-start(f32[6,192,128]{2,1,0:T(8,128)} %get-tuple-element.411), channel_id=1, source_target_pairs={{0,1},{1,0},{2,3},{3,2},{4,5},{5,4},{6,7},{7,6},{8,9},{9,8},{10,11... | collective-permute-start | bytes 1769480 | tf_op jit(solution)/shard_map/ppermute | solution.py:37
  30.4 41.9 %collective-permute-start.1 = (f32[6,192,128]{2,1,0:T(8,128)}, f32[6,192,128]{2,1,0:T(8,128)}, u32[]{:S(2)}, u32[]{:S(2)}) collective-permute-start(f32[6,192,128]{2,1,0:T(8,128)} %get-tuple-element.410), channel_id=1, source_target_pairs={{0,2},{1,3},{2,0},{3,1},{4,6},{5,7},{6,4},{7,5},{8,10},{9,11},{10,... | collective-permute-start | bytes 1769480 | tf_op jit(solution)/shard_map/ppermute | solution.py:37
  33.0 51.7 %collective-permute-start.2 = (f32[6,192,128]{2,1,0:T(8,128)}, f32[6,192,128]{2,1,0:T(8,128)}, u32[]{:S(2)}, u32[]{:S(2)}) collective-permute-start(f32[6,192,128]{2,1,0:T(8,128)} %get-tuple-element.409), channel_id=1, source_target_pairs={{0,3},{1,2},{2,1},{3,0},{4,7},{5,6},{6,5},{7,4},{8,11},{9,10},{10,... | collective-permute-start | bytes 1769480 | tf_op jit(solution)/shard_map/ppermute | solution.py:37
  33.1 53.5 %collective-permute-start.3 = (f32[6,192,128]{2,1,0:T(8,128)}, f32[6,192,128]{2,1,0:T(8,128)}, u32[]{:S(2)}, u32[]{:S(2)}) collective-permute-start(f32[6,192,128]{2,1,0:T(8,128)} %get-tuple-element.408), channel_id=1, source_target_pairs={{0,4},{1,5},{2,6},{3,7},{4,0},{5,1},{6,2},{7,3},{8,12},{9,13},{10,... | collective-permute-start | bytes 1769480 | tf_op jit(solution)/shard_map/ppermute | solution.py:37
  35.8 52.6 %collective-permute-start.4 = (f32[6,192,128]{2,1,0:T(8,128)S(1)}, f32[6,192,128]{2,1,0:T(8,128)}, u32[]{:S(2)}, u32[]{:S(2)}) collective-permute-start(f32[6,192,128]{2,1,0:T(8,128)S(1)} %get-tuple-element.407), channel_id=1, source_target_pairs={{0,5},{1,4},{2,7},{3,6},{4,1},{5,0},{6,3},{7,2},{8,13},{9,12},{10,... | collective-permute-start | bytes 1769480 | tf_op jit(solution)/shard_map/ppermute | solution.py:37
  38.4 150.9 %all-to-all-start = ((s32[1,1536,128]{2,0,1:T(1,128)}), s32[1,1536,128]{2,0,1:T(1,128)}, u32[]{:S(2)}, u32[]{:S(2)}) async-start(s32[1,1536,128]{2,0,1:T(1,128)} %bitcast.7), calls=%async_computation | async-start | bytes 1572864 | tf_op jit(solution)/shard_map/all_to_all | solution.py:194
  43.3 354.2 %all-reduce.7.cloned.1.call-start = ((), (), s32[]{:S(2)}) async-start(), calls=%async_computation.1 | async-start | bytes 3145728 | tf_op jit(solution)/shard_map/psum | solution.py:200
  45.5 67.7 %collective-permute-start.5 = (f32[6,192,128]{2,1,0:T(8,128)S(1)}, f32[6,192,128]{2,1,0:T(8,128)S(1)}, u32[]{:S(2)}, u32[]{:S(2)}) collective-permute-start(f32[6,192,128]{2,1,0:T(8,128)S(1)} %get-tuple-element.406), channel_id=1, source_target_pairs={{0,6},{1,7},{2,4},{3,5},{4,2},{5,3},{6,0},{7,1},{8,14},{9,15},{10,... | collective-permute-start | bytes 1769480 | tf_op jit(solution)/shard_map/ppermute | solution.py:37
  72.4 52.5 %collective-permute-start.6 = (f32[6,192,128]{2,1,0:T(8,128)S(1)}, f32[6,192,128]{2,1,0:T(8,128)S(1)}, u32[]{:S(2)}, u32[]{:S(2)}) collective-permute-start(f32[6,192,128]{2,1,0:T(8,128)S(1)} %get-tuple-element.405), channel_id=1, source_target_pairs={{0,7},{1,6},{2,5},{3,4},{4,3},{5,2},{6,1},{7,0},{8,15},{9,14},{10,... | collective-permute-start | bytes 1769480 | tf_op jit(solution)/shard_map/ppermute | solution.py:37
  131.2 5.3 slice-start
  131.2 5.3 slice-start.1
  306.4 105.7 %copy-start.9 = (s32[512]{0:T(512)S(1)}, s32[512]{0:T(512)}, u32[]{:S(2)}) copy-start(s32[512]{0:T(512)} %param.18) | copy-start | bytes 6148
  306.4 105.7 %copy-start.1 = (f32[512,128]{1,0:T(8,128)S(1)}, f32[512,128]{1,0:T(8,128)}, u32[]{:S(2)}) copy-start(f32[512,128]{1,0:T(8,128)} %param.13) | copy-start | bytes 786436
  306.4 152.5 %all-gather.2.cloned.1.call-start = ((), (), s32[]{:S(2)}) async-start(), calls=%async_computation.2 | async-start | bytes 4718592 | tf_op jit(solution)/shard_map/all_gather | solution.py:202
  518.0 3.7 copy-start
  518.0 3.7 copy-start.2
  518.0 3.8 copy-start.3
  518.0 3.9 copy-start.4
  518.0 3.9 copy-start.5
  518.0 4.0 copy-start.6
  526.6 4.7 collective-permute-start.7
  557.5 13.0 %copy-start.8 = (f32[4,512]{1,0:T(4,128)}, f32[4,512]{1,0:T(4,128)S(1)}, u32[]{:S(2)}) copy-start(f32[4,512]{1,0:T(4,128)S(1)} %pad_maximum_fusion.1) | copy-start | bytes 24580
  558.2 5.7 collective-permute-start.8
Sparse Core Ops, SparseCore 0:
  306.5 90.9 all-reduce.6
  412.0 46.8 all-gather.1
